TPU v7x, 32 devices: a whole 2x2x4 slice. The times are simulated.
32 devices in a mesh: vol: 8 (over z, y), pix: 4 (over x, core).
Axes of the slice: x: 2, y: 2, z: 4, core: 2. Of those that a mesh axis runs over, the one named last changes fastest.
Arguments:
- kernel: bfloat16 [524288, 128], P(('vol', 'pix')), may hold values from 0 to 0.25
- pressure: bfloat16 [524288], P(('vol', 'pix')), may hold values from 0.049804688 to 2
- velocity: bfloat16 [524288], P(('vol', 'pix')), may hold values from -4 to 4
- entry_slot: int32 [32, 16384], P(('vol', 'pix')), may hold values from 0 to 1023, never falling along the last dimension, each value on 1 to 32 neighbouring positions
- slot_tile: int32 [32, 1024], P(('vol', 'pix')), may hold values from 0 to 8191, as said below
- tile_owner: int32 [8192], replicated, may hold values from 0 to 3, as said below
Outputs:
- owned_tiles: float32 [16384, 256], P(('vol', 'pix'))
- shell_map: float32 [8192, 256], P('vol')
Inputs may be any that keep to these rules, and one draw needn't show every extreme that they name: `entry_slot`: for each device the slot numbers never fall along its 16384 crossings; every slot has at least one crossing and at most 32. `tile_owner`: within every block of 1024 consecutive tiles each pix index owns 256 // 2 to 512 tiles, and one owner of each block owns exactly 512. `slot_tile`: the 1024 tiles of one device are distinct; at most 64 of them belong to any one owning device (vol index t // 1024, pix index tile_owner[t]), and one owning device gets exactly 64 from every device.
All inputs are finite; a program needn't handle non-finite values.
Results may differ from a plain program's by a relative error of at most 0.0003.
Values sent between devices are 32-bit elements; how exact they have to be, the bound alone decides.
A program may use at most 64 MiB of HBM per device.

v0:
```python
import jax
import jax.numpy as jnp
from jax import lax
from jax.sharding import PartitionSpec as P


def project(kernel, pressure, velocity, entry_slot, slot_count):
    entry_count = kernel.shape[0]
    pixel_count = kernel.shape[1]
    block_rows = min(256, entry_count)
    block_count = entry_count // block_rows
    turn_count = min(16, block_count)
    group_size = block_count // turn_count
    within = jnp.arange(block_rows, dtype=jnp.int32)
    nothing = jnp.zeros((), kernel.dtype)

    def accumulate(running, inputs):
        kernel_weights, thermal, kinetic, slot_ids = inputs
        offsets = slot_ids[:, 0]
        local_slot = slot_ids - offsets[:, None]
        matches = within[None, :, None] == local_slot[:, None, :]
        particle_weights = jnp.stack(
            [
                jnp.where(matches, thermal[:, None, :], nothing),
                jnp.where(matches, kinetic[:, None, :], nothing),
            ],
            axis=2,
        )
        particle_weights = particle_weights.reshape(group_size, 2 * block_rows, block_rows)
        pixel_products = jnp.einsum(
            "vzc,vcx->vzx", particle_weights, kernel_weights, preferred_element_type=jnp.float32
        )
        pixel_products = pixel_products.reshape(group_size * block_rows, 2 * pixel_count)
        target_rows = (offsets[:, None] + within[None, :]).reshape(group_size * block_rows)
        return (running.at[target_rows].add(pixel_products), None)

    start_value = jnp.zeros((slot_count + block_rows, 2 * pixel_count), jnp.float32)
    inputs = (
        kernel.reshape(turn_count, group_size, block_rows, pixel_count),
        pressure.reshape(turn_count, group_size, block_rows),
        velocity.reshape(turn_count, group_size, block_rows),
        entry_slot.reshape(turn_count, group_size, block_rows),
    )
    result, unused = lax.scan(accumulate, start_value, inputs)
    return result[:slot_count]


def owner_rows(tile_owner, vol_count, pix_count):
    tile_count = tile_owner.shape[0]
    owners = tile_owner.reshape(vol_count, tile_count // vol_count)
    matches = owners[:, None, :] == jnp.arange(pix_count, dtype=jnp.int32)[None, :, None]
    owner_ranking = jnp.cumsum(matches.astype(jnp.int32), axis=2, dtype=jnp.int32) - 1
    return jnp.sum(jnp.where(matches, owner_ranking, 0), axis=1, dtype=jnp.int32).reshape(
        tile_count
    )


def shards(kernel, pressure, velocity, entry_slot, slot_tile, tile_owner):
    vol_count = lax.axis_size("vol")
    pix_count = lax.axis_size("pix")
    device_count = vol_count * pix_count
    slot_count = slot_tile.shape[1]
    tile_count = tile_owner.shape[0]
    block_tile_list = tile_count // vol_count
    owned_most = 2 * block_tile_list // pix_count
    bucket_size = 2 * slot_count // device_count
    partial_value = project(kernel, pressure, velocity, entry_slot[0], slot_count)
    tile_width = partial_value.shape[1]
    row_of_tile = owner_rows(tile_owner, vol_count, pix_count)
    targets = slot_tile[0]
    target_dev = targets // block_tile_list * pix_count + tile_owner[targets]
    target_row = row_of_tile[targets]
    labels = jnp.arange(device_count, dtype=jnp.int32)
    matches = labels[:, None] == target_dev[None, :]
    owner_ranking = jnp.cumsum(matches.astype(jnp.int32), axis=1, dtype=jnp.int32) - 1
    position = jnp.sum(jnp.where(matches, owner_ranking, 0), axis=0, dtype=jnp.int32)
    bucket = target_dev * bucket_size + position
    outgoing = (
        jnp.zeros((device_count * bucket_size, tile_width), jnp.float32)
        .at[bucket]
        .set(partial_value)
    )
    destined = (
        jnp.full((device_count * bucket_size,), owned_most, jnp.int32).at[bucket].set(target_row)
    )
    arrived, arrived_rows = (
        lax.all_to_all(
            outgoing.reshape(device_count, bucket_size, tile_width),
            ("vol", "pix"),
            split_axis=0,
            concat_axis=0,
            tiled=True,
        ),
        lax.all_to_all(
            destined.reshape(device_count, bucket_size),
            ("vol", "pix"),
            split_axis=0,
            concat_axis=0,
            tiled=True,
        ),
    )
    owned = jax.ops.segment_sum(
        arrived.reshape(-1, tile_width), arrived_rows.reshape(-1), num_segments=owned_most + 1
    )[:owned_most]
    volume_index = lax.axis_index("vol")
    block_owner = lax.dynamic_slice_in_dim(
        tile_owner, volume_index * block_tile_list, block_tile_list
    )
    block_row = lax.dynamic_slice_in_dim(
        row_of_tile, volume_index * block_tile_list, block_tile_list
    )
    source = block_owner * owned_most + block_row
    gathered_piece = lax.all_gather(owned, "pix", axis=0, tiled=True)
    piece_rows = gathered_piece.shape[0]
    inside = (source >= 0) & (source < piece_rows)
    taken = gathered_piece[jnp.clip(source, 0, piece_rows - 1)]
    shell_map = jnp.where(inside[:, None], taken, 0.0)
    return (owned, shell_map)


def solution(mesh):
    in_specs = (
        P(("vol", "pix"), None),
        P(("vol", "pix")),
        P(("vol", "pix")),
        P(("vol", "pix"), None),
        P(("vol", "pix"), None),
        P(),
    )
    out_specs = (P(("vol", "pix"), None), P("vol", None))
    return jax.shard_map(shards, mesh=mesh, in_specs=in_specs, out_specs=out_specs, check_vma=False)
```

profile of v0, /device:TPU:29, one launch (start us, length us, event | category | flops | bytes accessed | tf_op | source)
XLA Modules:
  0.0 417.5 jit_solution(17928445462744167664)
XLA Ops:
  13.8 9.0 %reduce-window.14 = s32[32,8,128]{2,1,0:T(8,128)S(1)} reduce-window(s32[32,8,128]{2,1,0:T(8,128)S(1)} %fusion.13, s32[]{:T(128)} %constant.37.clone.1), window={size=1x1x128 pad=0_0x0_0x127_0}, to_apply=%region_0.1 | reduce-window | flops 4161536 | bytes 262148 | tf_op jit(solution)/shard_map/reduce-window
  23.3 9.0 %reduce-window.16 = s32[8,4,8,128]{3,2,1,0:T(8,128)S(1)} reduce-window(s32[8,4,8,128]{3,2,1,0:T(8,128)S(1)} %fusion.12, s32[]{:T(128)} %constant.37.clone.1), window={size=1x1x1x128 pad=0_0x0_0x0_0x127_0}, to_apply=%region_3.4 | reduce-window | flops 4161536 | bytes 262148 | tf_op jit(solution)/shard_map/reduce-window.2
  44.7 6.2 %all-to-all-start = ((s32[32,1,64]{2,1,0:T(1,128)}), s32[32,1,64]{2,1,0:T(1,128)}, u32[]{:S(2)}, u32[]{:S(2)}) async-start(s32[32,1,64]{2,1,0:T(1,128)} %all_to_all.9), calls=%async_computation | async-start | bytes 32768 | tf_op jit(solution)/shard_map/all_to_all | solution.py:94
  53.6 254.5 %while.12 = (s32[]{:T(128)}, f32[1280,256]{1,0:T(8,128)S(1)}, s32[16,4,256]{2,1,0:T(4,128)S(1)}, bf16[16,4,256]{2,1,0:T(4,128)(2,1)}, bf16[16,4,256]{2,1,0:T(4,1...) while((s32[]{:T(128)}, f32[1280,256]{1,0:T(8,128)S(1)}, ...), condition=%wide.region_9.10_spmd.clone.clone, body=%wide.region_7.9_spmd.clone.clone.sunk | while | flops 137368576 | bytes 12902549 | solution.py:44
  63.0 6.5 %scatter_fusion = f32[1280,256]{1,0:T(8,128)S(1)} fusion(f32[1280,256]{1,0:T(8,128)S(1)} %get-tuple-element.150, s32[1024]{0:T(1024)S(1)} %bitcast.65, f32[1024,256]{1,0:T(8,128)S(1)} %reshape.369), kind=kCustom, calls=%fused_computation.3.clone.clone.1 | custom fusion | flops 262144 | bytes 3149824 | tf_op jit(solution)/shard_map/while/body/eval_jaxpr/scatter-add | solution.py:35
  78.9 6.5 %scatter_fusion = f32[1280,256]{1,0:T(8,128)S(1)} fusion(f32[1280,256]{1,0:T(8,128)S(1)} %get-tuple-element.150, s32[1024]{0:T(1024)S(1)} %bitcast.65, f32[1024,256]{1,0:T(8,128)S(1)} %reshape.369), kind=kCustom, calls=%fused_computation.3.clone.clone.1 | custom fusion | flops 262144 | bytes 3149824 | tf_op jit(solution)/shard_map/while/body/eval_jaxpr/scatter-add | solution.py:35
  94.8 6.5 %scatter_fusion = f32[1280,256]{1,0:T(8,128)S(1)} fusion(f32[1280,256]{1,0:T(8,128)S(1)} %get-tuple-element.150, s32[1024]{0:T(1024)S(1)} %bitcast.65, f32[1024,256]{1,0:T(8,128)S(1)} %reshape.369), kind=kCustom, calls=%fused_computation.3.clone.clone.1 | custom fusion | flops 262144 | bytes 3149824 | tf_op jit(solution)/shard_map/while/body/eval_jaxpr/scatter-add | solution.py:35
  110.7 6.5 %scatter_fusion = f32[1280,256]{1,0:T(8,128)S(1)} fusion(f32[1280,256]{1,0:T(8,128)S(1)} %get-tuple-element.150, s32[1024]{0:T(1024)S(1)} %bitcast.65, f32[1024,256]{1,0:T(8,128)S(1)} %reshape.369), kind=kCustom, calls=%fused_computation.3.clone.clone.1 | custom fusion | flops 262144 | bytes 3149824 | tf_op jit(solution)/shard_map/while/body/eval_jaxpr/scatter-add | solution.py:35
  126.6 6.5 %scatter_fusion = f32[1280,256]{1,0:T(8,128)S(1)} fusion(f32[1280,256]{1,0:T(8,128)S(1)} %get-tuple-element.150, s32[1024]{0:T(1024)S(1)} %bitcast.65, f32[1024,256]{1,0:T(8,128)S(1)} %reshape.369), kind=kCustom, calls=%fused_computation.3.clone.clone.1 | custom fusion | flops 262144 | bytes 3149824 | tf_op jit(solution)/shard_map/while/body/eval_jaxpr/scatter-add | solution.py:35
  142.5 6.5 %scatter_fusion = f32[1280,256]{1,0:T(8,128)S(1)} fusion(f32[1280,256]{1,0:T(8,128)S(1)} %get-tuple-element.150, s32[1024]{0:T(1024)S(1)} %bitcast.65, f32[1024,256]{1,0:T(8,128)S(1)} %reshape.369), kind=kCustom, calls=%fused_computation.3.clone.clone.1 | custom fusion | flops 262144 | bytes 3149824 | tf_op jit(solution)/shard_map/while/body/eval_jaxpr/scatter-add | solution.py:35
  158.4 6.5 %scatter_fusion = f32[1280,256]{1,0:T(8,128)S(1)} fusion(f32[1280,256]{1,0:T(8,128)S(1)} %get-tuple-element.150, s32[1024]{0:T(1024)S(1)} %bitcast.65, f32[1024,256]{1,0:T(8,128)S(1)} %reshape.369), kind=kCustom, calls=%fused_computation.3.clone.clone.1 | custom fusion | flops 262144 | bytes 3149824 | tf_op jit(solution)/shard_map/while/body/eval_jaxpr/scatter-add | solution.py:35
  174.3 6.5 %scatter_fusion = f32[1280,256]{1,0:T(8,128)S(1)} fusion(f32[1280,256]{1,0:T(8,128)S(1)} %get-tuple-element.150, s32[1024]{0:T(1024)S(1)} %bitcast.65, f32[1024,256]{1,0:T(8,128)S(1)} %reshape.369), kind=kCustom, calls=%fused_computation.3.clone.clone.1 | custom fusion | flops 262144 | bytes 3149824 | tf_op jit(solution)/shard_map/while/body/eval_jaxpr/scatter-add | solution.py:35
  190.2 6.5 %scatter_fusion = f32[1280,256]{1,0:T(8,128)S(1)} fusion(f32[1280,256]{1,0:T(8,128)S(1)} %get-tuple-element.150, s32[1024]{0:T(1024)S(1)} %bitcast.65, f32[1024,256]{1,0:T(8,128)S(1)} %reshape.369), kind=kCustom, calls=%fused_computation.3.clone.clone.1 | custom fusion | flops 262144 | bytes 3149824 | tf_op jit(solution)/shard_map/while/body/eval_jaxpr/scatter-add | solution.py:35
  206.2 6.5 %scatter_fusion = f32[1280,256]{1,0:T(8,128)S(1)} fusion(f32[1280,256]{1,0:T(8,128)S(1)} %get-tuple-element.150, s32[1024]{0:T(1024)S(1)} %bitcast.65, f32[1024,256]{1,0:T(8,128)S(1)} %reshape.369), kind=kCustom, calls=%fused_computation.3.clone.clone.1 | custom fusion | flops 262144 | bytes 3149824 | tf_op jit(solution)/shard_map/while/body/eval_jaxpr/scatter-add | solution.py:35
  222.1 6.5 %scatter_fusion = f32[1280,256]{1,0:T(8,128)S(1)} fusion(f32[1280,256]{1,0:T(8,128)S(1)} %get-tuple-element.150, s32[1024]{0:T(1024)S(1)} %bitcast.65, f32[1024,256]{1,0:T(8,128)S(1)} %reshape.369), kind=kCustom, calls=%fused_computation.3.clone.clone.1 | custom fusion | flops 262144 | bytes 3149824 | tf_op jit(solution)/shard_map/while/body/eval_jaxpr/scatter-add | solution.py:35
  238.0 6.5 %scatter_fusion = f32[1280,256]{1,0:T(8,128)S(1)} fusion(f32[1280,256]{1,0:T(8,128)S(1)} %get-tuple-element.150, s32[1024]{0:T(1024)S(1)} %bitcast.65, f32[1024,256]{1,0:T(8,128)S(1)} %reshape.369), kind=kCustom, calls=%fused_computation.3.clone.clone.1 | custom fusion | flops 262144 | bytes 3149824 | tf_op jit(solution)/shard_map/while/body/eval_jaxpr/scatter-add | solution.py:35
  253.9 6.5 %scatter_fusion = f32[1280,256]{1,0:T(8,128)S(1)} fusion(f32[1280,256]{1,0:T(8,128)S(1)} %get-tuple-element.150, s32[1024]{0:T(1024)S(1)} %bitcast.65, f32[1024,256]{1,0:T(8,128)S(1)} %reshape.369), kind=kCustom, calls=%fused_computation.3.clone.clone.1 | custom fusion | flops 262144 | bytes 3149824 | tf_op jit(solution)/shard_map/while/body/eval_jaxpr/scatter-add | solution.py:35
  269.8 6.5 %scatter_fusion = f32[1280,256]{1,0:T(8,128)S(1)} fusion(f32[1280,256]{1,0:T(8,128)S(1)} %get-tuple-element.150, s32[1024]{0:T(1024)S(1)} %bitcast.65, f32[1024,256]{1,0:T(8,128)S(1)} %reshape.369), kind=kCustom, calls=%fused_computation.3.clone.clone.1 | custom fusion | flops 262144 | bytes 3149824 | tf_op jit(solution)/shard_map/while/body/eval_jaxpr/scatter-add | solution.py:35
  285.7 6.5 %scatter_fusion = f32[1280,256]{1,0:T(8,128)S(1)} fusion(f32[1280,256]{1,0:T(8,128)S(1)} %get-tuple-element.150, s32[1024]{0:T(1024)S(1)} %bitcast.65, f32[1024,256]{1,0:T(8,128)S(1)} %reshape.369), kind=kCustom, calls=%fused_computation.3.clone.clone.1 | custom fusion | flops 262144 | bytes 3149824 | tf_op jit(solution)/shard_map/while/body/eval_jaxpr/scatter-add | solution.py:35
  301.6 6.5 %scatter_fusion = f32[1280,256]{1,0:T(8,128)S(1)} fusion(f32[1280,256]{1,0:T(8,128)S(1)} %get-tuple-element.150, s32[1024]{0:T(1024)S(1)} %bitcast.65, f32[1024,256]{1,0:T(8,128)S(1)} %reshape.369), kind=kCustom, calls=%fused_computation.3.clone.clone.1 | custom fusion | flops 262144 | bytes 3149824 | tf_op jit(solution)/shard_map/while/body/eval_jaxpr/scatter-add | solution.py:35
  308.2 6.3 %scatter_custom_fusion.2 = f32[2048,256]{1,0:T(8,128)} fusion(s32[1024]{0:T(1024)S(1)} %bitcast.78, f32[1280,256]{1,0:T(8,128)S(1)} %get-tuple-element.42, f32[]{:T(128)} %constant.27.clone.1), kind=kCustom, calls=%fused_computation.23 | custom fusion | bytes 3145732 | tf_op jit(solution)/shard_map/scatter | solution.py:81
  321.8 44.9 %all-to-all-done.1 = f32[32,64,256]{2,1,0:T(8,128)S(1)} async-done(((f32[32,64,256]{2,1,0:T(8,128)}), f32[32,64,256]{2,1,0:T(8,128)S(1)}, u32[]{:S(2)}, u32[]{:S(2)}) %all-to-all-start.1) | async-done | bytes 2097184 | tf_op jit(solution)/shard_map/all_to_all | solution.py:87
  366.7 12.6 %scatter_custom_fusion.3 = f32[513,256]{1,0:T(8,128)S(1)} fusion(s32[2048]{0:T(1024)S(1)} %reshape.326, f32[2048,256]{1,0:T(8,128)S(1)} %bitcast.64, f32[]{:T(128)} %constant.27.clone.1), kind=kCustom, calls=%fused_computation.27 | custom fusion | flops 524288 | bytes 525316 | tf_op jit(solution)/shard_map/scatter-add | solution.py:102
  380.2 24.2 %all-gather.2.cloned.1.call-done = f32[2048,256]{1,0:T(8,128)} async-done(((f32[512,256]{1,0:T(8,128)}), f32[2048,256]{1,0:T(8,128)}) %all-gather.2.cloned.1.call-update) | async-done | bytes 2097168 | tf_op jit(solution)/shard_map/all_gather | solution.py:113
  (224 shorter events, 185.3 us)
Async XLA Ops:
  7.9 5.9 %copy-start.2 = (s32[1,1024]{1,0:T(1,128)S(1)}, s32[1,1024]{1,0:T(1,128)}, u32[]{:S(2)}) copy-start(s32[1,1024]{1,0:T(1,128)} %param.12) | copy-start | bytes 12292
  7.9 15.4 %copy-start = (s32[8192]{0:T(1024)S(1)}, s32[8192]{0:T(1024)}, u32[]{:S(2)}) copy-start(s32[8192]{0:T(1024)} %param.13) | copy-start | bytes 98308
  33.5 17.5 %copy-start.3 = (bf16[16384]{0:T(1024)(128)(2,1)S(1)}, bf16[16384]{0:T(1024)(128)(2,1)}, u32[]{:S(2)}) copy-start(bf16[16384]{0:T(1024)(128)(2,1)} %param.9) | copy-start | bytes 98308
  33.5 18.1 %copy-start.4 = (bf16[16384]{0:T(1024)(128)(2,1)S(1)}, bf16[16384]{0:T(1024)(128)(2,1)}, u32[]{:S(2)}) copy-start(bf16[16384]{0:T(1024)(128)(2,1)} %param.10) | copy-start | bytes 98308
  33.5 19.2 %copy-start.1 = (s32[1,16384]{1,0:T(1,128)S(1)}, s32[1,16384]{1,0:T(1,128)}, u32[]{:S(2)}) copy-start(s32[1,16384]{1,0:T(1,128)} %param.11) | copy-start | bytes 196612
  44.7 269.8 %all-to-all-start = ((s32[32,1,64]{2,1,0:T(1,128)}), s32[32,1,64]{2,1,0:T(1,128)}, u32[]{:S(2)}, u32[]{:S(2)}) async-start(s32[32,1,64]{2,1,0:T(1,128)} %all_to_all.9), calls=%async_computation | async-start | bytes 32768 | tf_op jit(solution)/shard_map/all_to_all | solution.py:94
  314.5 52.3 %all-to-all-start.1 = ((f32[32,64,256]{2,1,0:T(8,128)}), f32[32,64,256]{2,1,0:T(8,128)S(1)}, u32[]{:S(2)}, u32[]{:S(2)}) async-start(f32[32,64,256]{2,1,0:T(8,128)} %bitcast.12), calls=%async_computation.1 | async-start | bytes 4194304 | tf_op jit(solution)/shard_map/all_to_all | solution.py:87
  320.3 84.1 %all-gather.2.cloned.1.call-start = ((), (), s32[]{:S(2)}) async-start(), calls=%async_computation.2 | async-start | bytes 2621440 | tf_op jit(solution)/shard_map/all_gather | solution.py:113
Sparse Core Ops, SparseCore 0:
  380.3 24.1 all-gather.1
where the time goes:
time: 421 us; the launch traced here: 418 us
  other arithmetic  207 us (49%)
  local copies, waits for them, and re-layouts  76.7 us (18%)
  waiting for transfers between devices  69.2 us (16%)
  matrix products  37.8 us (9%)
  between operations  14.3 us (3%)
  starting transfers between devices  12.1 us (3%)
    scatter-add x16, other arithmetic, accumulate(): return (running.at[target_rows].add(pixel_products), None)  105 us
    all_to_all x1, waiting for transfers between devices, shards(): lax.all_to_all(outgoing.reshape(device_count, bucket_size, tile_width), (...  44.9 us
    another operation x16, other arithmetic, accumulate(): jnp.stack([jnp.where(matches, thermal[:, None, :], nothing), jnp.where(ma...  38.9 us
    dot_general x16, matrix products, accumulate(): jnp.einsum('vzc,vcx->vzx', particle_weights, kernel_weights, preferred_el...  37.8 us
    select_n x16, other arithmetic, accumulate(): jnp.where(matches, thermal[:, None, :], nothing)  25.9 us
    reshape x16, local copies, waits for them, and re-layouts, accumulate(): pixel_products.reshape(group_size * block_rows, 2 * pixel_count)  24.6 us
    all_gather x1, waiting for transfers between devices, shards(): gathered_piece = lax.all_gather(owned, 'pix', axis=0, tiled=True)  24.2 us
    another operation x4, other arithmetic  18.7 us
  transfers between devices with their start and end apart: 3, of which 2 were waited for; matrix products, arithmetic and copies ran while one was open for 63% of the time, Pallas kernels for 0%

commit v1 on v0

v1 whole, which is shorter than its diff:
```python
import functools

import jax
import jax.numpy as jnp
from jax import lax
from jax.experimental import pallas as pl
from jax.experimental.pallas import tpu as pltpu
from jax.sharding import PartitionSpec as P

MESH = pl.DeviceIdType.MESH
LANES = 128
BLOCK = 256
WINDOW = 48
F32 = jnp.float32
BF16 = jnp.bfloat16
I32 = jnp.int32


def iota(shape, axis):
    return lax.broadcasted_iota(I32, shape, axis)


def onehot(mask):
    return jnp.where(mask, 1.0, 0.0).astype(BF16)


def dot(a, b):
    return jnp.dot(a, b, preferred_element_type=F32)


def halves(x):
    high = x.astype(BF16)
    low = (x - high.astype(F32)).astype(BF16)
    return jnp.concatenate([high, low], axis=1)


def prepare(
    dims, base_ref, last_ref, kern_hbm, thermal_ref, kinetic_ref, slot_ref, tile_ref, owner_ref,
    out_ref, ids_ref, code_ref, kern_ref, thermal32, kinetic32, part_ref, split_ref, sems,
):
    vol_count, pix_count, slots, block_tiles, owned_most, cap = dims
    device_count = vol_count * pix_count
    entries = kern_ref.shape[0]
    blocks = entries // BLOCK
    pieces = sems.shape[0]
    piece = entries // pieces

    def fetch(q):
        rows = pl.ds(q * piece, piece)
        return pltpu.make_async_copy(kern_hbm.at[rows], kern_ref.at[rows], sems.at[q])

    for q in range(pieces):
        fetch(q).start()

    high_count = owner_ref.shape[0]
    block_high = block_tiles // LANES
    owner = jnp.transpose(owner_ref[...].astype(F32))
    lower = onehot(iota((LANES, LANES), 1) < iota((LANES, LANES), 0))
    first, second = iota((high_count, high_count), 0), iota((high_count, high_count), 1)
    before = onehot((first < second) & (first // block_high == second // block_high))
    rank = jnp.zeros((LANES, high_count), F32)
    for p in range(pix_count):
        mine = owner == p
        ones = jnp.where(mine, 1.0, 0.0)
        inside = dot(lower, ones.astype(BF16))
        total = jnp.broadcast_to(jnp.sum(ones, axis=0, keepdims=True), (8, high_count))
        ahead = dot(total.astype(BF16), before)[0:1]
        rank = rank + jnp.where(mine, inside + ahead, 0.0)

    code = owner * owned_most + rank
    first_high = lax.axis_index("vol") * block_high
    lane = iota((LANES, high_count), 1)
    for h in range(block_high):
        column = jnp.sum(jnp.where(lane == first_high + h, code, 0.0), axis=1, keepdims=True)
        code_ref[h * LANES:(h + 1) * LANES, :] = jnp.broadcast_to(
            column, (LANES, LANES)
        ).astype(I32)

    parts = max(1, owned_most // 256)
    rank_high = jnp.floor(rank * (1.0 / 256.0))
    rank_low = rank - 256.0 * rank_high
    table = jnp.concatenate([owner * parts + rank_high, rank_low], axis=0).astype(BF16)
    tile = tile_ref[...]
    high, low = tile // LANES, tile % LANES
    found = dot(table, onehot(iota((high_count, slots), 0) == high))
    pick = iota((LANES, slots), 0) == low
    both = jnp.sum(jnp.where(pick, found[:LANES], 0.0), axis=0, keepdims=True).astype(I32)
    row_low = jnp.sum(jnp.where(pick, found[LANES:], 0.0), axis=0, keepdims=True)
    slot_owner = both // parts
    row_high = (both - slot_owner * parts).astype(F32)
    target = high // block_high * pix_count + slot_owner
    to_device = iota((device_count, slots), 0) == target
    ones = jnp.where(to_device, 1.0, 0.0)
    upper = onehot(iota((LANES, LANES), 0) < iota((LANES, LANES), 1))
    carry = jnp.zeros((device_count, 1), F32)
    position = []
    for j in range(slots // LANES):
        chunk = ones[:, j * LANES:(j + 1) * LANES]
        ranks = dot(chunk.astype(BF16), upper) + carry
        position.append(jnp.sum(chunk * ranks, axis=0, keepdims=True))
        carry = carry + jnp.sum(chunk, axis=1, keepdims=True)
    position = jnp.concatenate(position, axis=1).astype(I32)
    bucket = target * cap + position

    places = onehot(iota((LANES, slots), 0) % cap == position)
    values = jnp.concatenate(
        [jnp.where(to_device, row_high, 0.0), jnp.where(to_device, row_low + 1.0, 0.0)], axis=0
    )
    placed = lax.dot_general(
        values.astype(BF16), places, (((1,), (1,)), ((), ())), preferred_element_type=F32
    )
    rows = placed[:device_count] * 256.0 + placed[device_count:] - 1.0
    ids_ref[...] = jnp.broadcast_to(
        rows.astype(I32)[:, None, :], (device_count, 8, LANES)
    )

    thermal32[...] = thermal_ref[...].astype(F32)
    kinetic32[...] = kinetic_ref[...].astype(F32)
    part_ref[...] = jnp.zeros_like(part_ref)
    within = iota((WINDOW, BLOCK), 0)

    def add_window(i, base):
        def pair(ref):
            return jnp.concatenate([ref[pl.ds(2 * i, 1), :], ref[pl.ds(2 * i + 1, 1), :]], axis=1)

        base = pl.multiple_of(base, 8)
        match = within + base == pair(slot_ref)
        weights = jnp.concatenate(
            [jnp.where(match, pair(thermal32), 0.0), jnp.where(match, pair(kinetic32), 0.0)], axis=0
        ).astype(BF16)
        sums = dot(weights, kern_ref[pl.ds(pl.multiple_of(i * BLOCK, BLOCK), BLOCK), :])
        part_ref[pl.ds(base, WINDOW), 0:LANES] += sums[:WINDOW]
        part_ref[pl.ds(base, WINDOW), LANES:2 * LANES] += sums[WINDOW:]

    per = blocks // pieces
    for q in range(pieces):
        fetch(q).wait()

        def first_window(i, unused):
            add_window(i, base_ref[i])
            return unused

        lax.fori_loop(q * per, (q + 1) * per, first_window, 0, unroll=4)

    def more_windows(i, unused):
        base = base_ref[i]
        extra = (last_ref[i] - base) // WINDOW

        def one(w, unused):
            add_window(i, base + w * WINDOW)
            return unused

        return lax.fori_loop(1, extra + 1, one, unused)

    lax.fori_loop(0, blocks, more_windows, 0)

    split_ref[...] = halves(part_ref[0:slots, :])
    some = min(256, device_count * cap)

    def permute(i, unused):
        start = pl.multiple_of(i * some, some)
        moved = dot(onehot(iota((some, slots), 0) + start == bucket), split_ref[...])
        out_ref[pl.ds(start, some), :] = moved[:, :2 * LANES] + moved[:, 2 * LANES:]
        return unused

    lax.fori_loop(0, device_count * cap // some, permute, 0)


def exchange(
    dims, out_hbm, ids_hbm, code_ref, owned_ref, shell_ref, arrived, ids, gathered,
    send_sem, recv_sem, ids_send, ids_recv, local_sem, own_send, own_recv, far_send, far_recv,
    pass_send, pass_recv,
):
    vol_count, pix_count, slots, block_tiles, owned_most, cap = dims
    device_count = vol_count * pix_count
    vol, pix = lax.axis_index("vol"), lax.axis_index("pix")
    me = vol * pix_count + pix
    width = 2 * LANES

    def peer(k):
        other_vol = (vol + k // pix_count) % vol_count
        other_pix = (pix + k % pix_count) % pix_count
        return other_vol, other_pix

    barrier = pltpu.get_barrier_semaphore()

    def greet(k, unused):
        pl.semaphore_signal(barrier, inc=1, device_id=peer(k), device_id_type=MESH)
        return unused

    lax.fori_loop(1, device_count, greet, 0)
    pl.semaphore_wait(barrier, device_count - 1)

    def ids_copy(k):
        other_vol, other_pix = peer(k)
        return pltpu.make_async_remote_copy(
            src_ref=ids_hbm.at[other_vol * pix_count + other_pix], dst_ref=ids.at[me],
            send_sem=ids_send.at[k], recv_sem=ids_recv.at[k],
            device_id=(other_vol, other_pix), device_id_type=MESH,
        )

    def rows_copy(k):
        other_vol, other_pix = peer(k)
        return pltpu.make_async_remote_copy(
            src_ref=out_hbm.at[pl.ds((other_vol * pix_count + other_pix) * cap, cap)],
            dst_ref=arrived.at[pl.ds(me * cap, cap)],
            send_sem=send_sem.at[k], recv_sem=recv_sem.at[k],
            device_id=(other_vol, other_pix), device_id_type=MESH,
        )

    def send(k, unused):
        ids_copy(k).start()
        rows_copy(k).start()
        return unused

    lax.fori_loop(1, device_count, send, 0)
    local_ids = pltpu.make_async_copy(ids_hbm.at[me], ids.at[me], local_sem.at[0])
    local_rows = pltpu.make_async_copy(
        out_hbm.at[pl.ds(me * cap, cap)], arrived.at[pl.ds(me * cap, cap)], local_sem.at[1]
    )
    local_ids.start()
    local_rows.start()
    local_ids.wait()
    local_rows.wait()

    group = pix_count * cap
    share = LANES // cap
    own = gathered.at[pix]
    own[...] = jnp.zeros((owned_most, width), F32)
    lane_part = iota((1, LANES), 1) // cap

    def receive(i, unused):
        def one(j, unused):
            k = i * pix_count + j
            ids_copy(k).wait_recv()
            rows_copy(k).wait_recv()
            return unused

        lax.fori_loop(jnp.where(i == 0, 1, 0), pix_count, one, 0)
        sender = (vol + vol_count - i) % vol_count
        pieces = []
        for tau in range(group // LANES):
            piece = jnp.full((1, LANES), -1, I32)
            for g in range(share):
                line = ids[sender * pix_count + tau * share + g]
                piece = jnp.where(lane_part == g, line[0:1], piece)
            pieces.append(piece)
        rows = jnp.concatenate(pieces, axis=1) if len(pieces) > 1 else pieces[0]
        places = onehot(iota((owned_most, group), 0) == rows)
        start = pl.multiple_of(sender * group, group)
        moved = dot(places, halves(arrived[pl.ds(start, group), :]))
        own[...] += moved[:, :width] + moved[:, width:]
        return unused

    lax.fori_loop(0, vol_count, receive, 0)

    core = pix % 2
    sibling = (vol, pix - core + (1 - core))
    far_count = pix_count // 2 - 1
    quarter_count = far_send.shape[1]
    quarter = owned_most // quarter_count

    def far_copy(k, q):
        to = (pix + 2 * k) % pix_count
        rows = pl.ds(q * quarter, quarter)
        return pltpu.make_async_remote_copy(
            src_ref=gathered.at[pix, rows], dst_ref=gathered.at[pix, rows],
            send_sem=far_send.at[k, q], recv_sem=far_recv.at[k, q],
            device_id=(vol, to), device_id_type=MESH,
        )

    def pass_copy(k, q):
        source = (pix + pix_count - 2 * k) % pix_count
        rows = pl.ds(q * quarter, quarter)
        return pltpu.make_async_remote_copy(
            src_ref=gathered.at[source, rows], dst_ref=gathered.at[source, rows],
            send_sem=pass_send.at[k, q], recv_sem=pass_recv.at[k, q],
            device_id=sibling, device_id_type=MESH,
        )

    own_copy = pltpu.make_async_remote_copy(
        src_ref=gathered.at[pix], dst_ref=gathered.at[pix],
        send_sem=own_send.at[0], recv_sem=own_recv.at[0],
        device_id=sibling, device_id_type=MESH,
    )
    for q in range(quarter_count):
        for k in range(1, far_count + 1):
            far_copy(k, q).start()
    own_copy.start()
    owned_ref[...] = own[...]

    def gather(p, start):
        data = halves(gathered[p])

        def one(h, unused):
            at = pl.ds(pl.multiple_of(h * LANES, LANES), LANES)
            codes = code_ref[at, :] - p * owned_most
            places = jnp.concatenate(
                [
                    onehot(codes == iota((LANES, LANES), 1) + r * LANES)
                    for r in range(owned_most // LANES)
                ],
                axis=1,
            )
            moved = dot(places, data)
            moved = moved[:, :width] + moved[:, width:]
            if start:
                shell_ref[at, :] = moved
            else:
                shell_ref[at, :] += moved
            return unused

        lax.fori_loop(0, block_tiles // LANES, one, 0)

    gather(pix, True)
    for q in range(quarter_count):
        for k in range(1, far_count + 1):
            far_copy(k, q).wait_recv()
            pass_copy(k, q).start()
    own_copy.wait_recv()
    gather(sibling[1], False)
    for k in range(1, far_count + 1):
        gather((pix + pix_count - 2 * k) % pix_count, False)
        for q in range(quarter_count):
            pass_copy(k, q).wait_recv()
        gather((sibling[1] + pix_count - 2 * k) % pix_count, False)

    own_copy.wait_send()
    for q in range(quarter_count):
        for k in range(1, far_count + 1):
            far_copy(k, q).wait_send()
            pass_copy(k, q).wait_send()

    def sent(k, unused):
        ids_copy(k).wait_send()
        rows_copy(k).wait_send()
        return unused

    lax.fori_loop(1, device_count, sent, 0)


def shards(kernel, pressure, velocity, entry_slot, slot_tile, tile_owner):
    vol_count, pix_count = lax.axis_size("vol"), lax.axis_size("pix")
    device_count = vol_count * pix_count
    entries = kernel.shape[0]
    slots = slot_tile.shape[1]
    tiles = tile_owner.shape[0]
    block_tiles = tiles // vol_count
    owned_most = 2 * block_tiles // pix_count
    cap = 2 * slots // device_count
    width = 2 * kernel.shape[1]
    dims = (vol_count, pix_count, slots, block_tiles, owned_most, cap)
    vmem = pl.BlockSpec(memory_space=pltpu.VMEM)
    smem = pl.BlockSpec(memory_space=pltpu.SMEM)
    anywhere = pl.BlockSpec(memory_space=pl.ANY)
    dma = pltpu.SemaphoreType.DMA

    ends = entry_slot.reshape(entries // BLOCK, BLOCK)
    base = ends[:, 0] // 8 * 8
    last = ends[:, BLOCK - 1]
    shape = (entries // LANES, LANES)
    outgoing, ids, codes = pl.pallas_call(
        functools.partial(prepare, dims),
        out_shape=(
            jax.ShapeDtypeStruct((device_count * cap, width), F32),
            jax.ShapeDtypeStruct((device_count, 8, LANES), I32),
            jax.ShapeDtypeStruct((block_tiles, LANES), I32),
        ),
        in_specs=[smem, smem, anywhere, vmem, vmem, vmem, vmem, vmem],
        out_specs=(vmem, vmem, vmem),
        scratch_shapes=[
            pltpu.VMEM(kernel.shape, BF16),
            pltpu.VMEM(shape, F32),
            pltpu.VMEM(shape, F32),
            pltpu.VMEM((slots + WINDOW, width), F32),
            pltpu.VMEM((slots, 2 * width), BF16),
            dma((4,)),
        ],
        name="prepare",
    )(
        base, last, kernel, pressure.reshape(shape), velocity.reshape(shape),
        entry_slot.reshape(shape), slot_tile, tile_owner.reshape(tiles // LANES, LANES),
    )

    quarters = 4
    chips = pix_count // 2
    return pl.pallas_call(
        functools.partial(exchange, dims),
        out_shape=(
            jax.ShapeDtypeStruct((owned_most, width), F32),
            jax.ShapeDtypeStruct((block_tiles, width), F32),
        ),
        in_specs=[anywhere, anywhere, vmem],
        out_specs=(vmem, vmem),
        scratch_shapes=[
            pltpu.VMEM((device_count * cap, width), F32),
            pltpu.VMEM((device_count, 8, LANES), I32),
            pltpu.VMEM((pix_count, owned_most, width), F32),
            dma((device_count,)), dma((device_count,)), dma((device_count,)), dma((device_count,)),
            dma((2,)), dma((1,)), dma((1,)),
            dma((chips, quarters)), dma((chips, quarters)),
            dma((chips, quarters)), dma((chips, quarters)),
        ],
        compiler_params=pltpu.CompilerParams(collective_id=0, has_side_effects=True),
        name="exchange",
    )(outgoing, ids, codes)


def solution(mesh):
    in_specs = (
        P(("vol", "pix"), None),
        P(("vol", "pix")),
        P(("vol", "pix")),
        P(("vol", "pix"), None),
        P(("vol", "pix"), None),
        P(),
    )
    out_specs = (P(("vol", "pix"), None), P("vol", None))
    return jax.shard_map(shards, mesh=mesh, in_specs=in_specs, out_specs=out_specs, check_vma=False)
```

time: 421 us -> 99.2 us (0.24)
  other arithmetic: 207 us -> 2.2 us
  Pallas kernels: 0 us -> 90.5 us
  local copies, waits for them, and re-layouts: 76.7 us -> 5.41 us
  waiting for transfers between devices: 69.2 us -> 0 us
  matrix products: 37.8 us -> 0 us
  between operations: 14.3 us -> 0.66 us
  starting transfers between devices: 12.1 us -> 0 us
    scatter-add x17 -> x0, other arithmetic: 117 us -> none  [the longest x16 105 us: accumulate(): return (running.at[target_rows].add(pixel_products), None)]
    pallas_call x0 -> x2, Pallas kernels: none -> 90.5 us  [the longest x1 78.3 us: shards(): pl.pallas_call(functools.partial(exchange, dims), out_shape=(jax.ShapeDty...]
    another operation x20 -> x0, other arithmetic: 57.6 us -> none  [the longest x16 38.9 us: accumulate(): jnp.stack([jnp.where(matches, thermal[:, None, :], nothing), jnp.where(ma...]
    all_to_all x2 -> x0, waiting for transfers between devices: 44.9 us -> none  [the longest x1 44.9 us: shards(): lax.all_to_all(outgoing.reshape(device_count, bucket_size, tile_width), (...]
    dot_general x16 -> x0, matrix products: 37.8 us -> none  [accumulate(): jnp.einsum('vzc,vcx->vzx', particle_weights, kernel_weights, preferred_el...]
    reshape x34 -> x1, local copies, waits for them, and re-layouts: 32.9 us -> 0.02 us  [shards(): ends = entry_slot.reshape(entries // BLOCK, BLOCK)]
    select_n x35 -> x0, other arithmetic: 28 us -> none  [the longest x16 25.9 us: accumulate(): jnp.where(matches, thermal[:, None, :], nothing)]
    all_gather x1 -> x0, waiting for transfers between devices: 24.2 us -> none  [shards(): gathered_piece = lax.all_gather(owned, 'pix', axis=0, tiled=True)]
  transfers between devices with their start and end apart: 3 -> 0, of which waited for: 2 -> 0; matrix products, arithmetic and copies ran while one was open for 63% -> 0% of each run, Pallas kernels for 0% -> 0%
where the time goes in v1:
time: 99.2 us; the launch traced here: 98.8 us
  Pallas kernels  90.5 us (91%)
  local copies, waits for them, and re-layouts  5.41 us (5%)
  other arithmetic  2.2 us (2%)
    pallas_call x1, Pallas kernels, shards(): pl.pallas_call(functools.partial(exchange, dims), out_shape=(jax.ShapeDty...  78.3 us
    pallas_call x1, Pallas kernels, shards(): pl.pallas_call(functools.partial(prepare, dims), out_shape=(jax.ShapeDtyp...  12.2 us
    unnamed x5, local copies, waits for them, and re-layouts  5.31 us

profile of v1, /device:TPU:29, one launch (start us, length us, event | category | flops | bytes accessed | tf_op | source)
XLA Modules:
  0.0 98.8 jit_solution(5754944930242618125)
XLA Ops:
  0.6 0.5 broadcast.12
  1.1 1.6 %reduce.3 = s32[16384]{0:T(1024)S(1)} reduce(s32[1,16384]{1,0:T(1,128)} %param.9, s32[]{:T(128)} %broadcast.12), dimensions={0}, to_apply=%param.9.reduce_sub_computation.3 | reduce | bytes 131076 | tf_op args[3]
  2.8 0.1 fusion.1
  2.9 0.6 copy.11
  3.5 0.1 copy.10
  3.6 0.6 fusion.base_ref
  4.1 12.2 %prepare.1 = (f32[2048,256]{1,0:T(8,128)}, s32[32,8,128]{2,1,0:T(8,128)}, s32[1024,128]{1,0:T(8,128)}) custom-call(s32[64]{0:T(128)} %fusion.base_ref, s32[64]{0:T(128)} %bitcast.19, bf16[16384,128]{1,0:T(8,128)(2,1)} %kern_hbm.1, bf16[128,128]{1,0:T(8,128)(2,1)} %bitcast.16, bf16[128,128]{1,0:T(8,128)(2,1)} %bitcast.17, s32[128,128]{1,0:T(8,128)} %bitcast.15, ...), custom_call_target="tpu_custom_call" | custom-call | tf_op jit(solution)/shard_map/prepare/pallas_call | solution.py:362
  16.3 78.3 %exchange.1 = (f32[512,256]{1,0:T(8,128)}, f32[1024,256]{1,0:T(8,128)}) custom-call(f32[2048,256]{1,0:T(8,128)} %get-tuple-element.5.out_hbm, s32[32,8,128]{2,1,0:T(8,128)} %get-tuple-element.6.ids_hbm, s32[1024,128]{1,0:T(8,128)} %get-tuple-element.7.code_ref), custom_call_target="tpu_custom_call" | custom-call | tf_op jit(solution)/shard_map/exchange/pallas_call | solution.py:387
  94.7 1.9 %copy.14 = f32[512,256]{1,0:T(8,128)} copy(f32[512,256]{1,0:T(8,128)} %get-tuple-element.12) | data formatting | bytes 1048576
  96.5 2.3 %copy.15 = f32[1024,256]{1,0:T(8,128)} copy(f32[1024,256]{1,0:T(8,128)} %get-tuple-element.13) | data formatting | bytes 2097152
  (1 shorter events, 0.0 us)

commit v2 on v1

--- a/solution.py
+++ b/solution.py
@@ -36,7 +36,8 @@
 
 def prepare(
     dims, base_ref, last_ref, kern_hbm, thermal_ref, kinetic_ref, slot_ref, tile_ref, owner_ref,
-    out_ref, ids_ref, code_ref, kern_ref, thermal32, kinetic32, part_ref, split_ref, sems,
+    out_ref, ids_ref, code_ref, kern_ref, thermal32, kinetic32, part_ref, split_ref, all_codes,
+    sems,
 ):
     vol_count, pix_count, slots, block_tiles, owned_most, cap = dims
     device_count = vol_count * pix_count
@@ -67,14 +68,9 @@
         ahead = dot(total.astype(BF16), before)[0:1]
         rank = rank + jnp.where(mine, inside + ahead, 0.0)
 
-    code = owner * owned_most + rank
-    first_high = lax.axis_index("vol") * block_high
-    lane = iota((LANES, high_count), 1)
-    for h in range(block_high):
-        column = jnp.sum(jnp.where(lane == first_high + h, code, 0.0), axis=1, keepdims=True)
-        code_ref[h * LANES:(h + 1) * LANES, :] = jnp.broadcast_to(
-            column, (LANES, LANES)
-        ).astype(I32)
+    all_codes[...] = jnp.transpose(owner * owned_most + rank).astype(I32)
+    first_high = pl.multiple_of(lax.axis_index("vol") * block_high, block_high)
+    code_ref[...] = all_codes[pl.ds(first_high, block_high), :]
 
     parts = max(1, owned_most // 256)
     rank_high = jnp.floor(rank * (1.0 / 256.0))
@@ -167,20 +163,21 @@
 
 
 def exchange(
-    dims, out_hbm, ids_hbm, code_ref, owned_ref, shell_ref, arrived, ids, gathered,
-    send_sem, recv_sem, ids_send, ids_recv, local_sem, own_send, own_recv, far_send, far_recv,
-    pass_send, pass_recv,
+    dims, out_hbm, ids_hbm, code_ref, owned_ref, shell_ref, arrived, ids, sums, crossed, gathered,
+    send_sem, recv_sem, ids_send, ids_recv, local_sem, mid_send, mid_recv, own_send, own_recv,
+    far_send, far_recv, pass_send, pass_recv,
 ):
     vol_count, pix_count, slots, block_tiles, owned_most, cap = dims
-    device_count = vol_count * pix_count
+    half = vol_count // 2
+    near_count = half * pix_count
     vol, pix = lax.axis_index("vol"), lax.axis_index("pix")
-    me = vol * pix_count + pix
+    side, place = vol // half, vol % half
+    mine = place * pix_count + pix
+    across = (vol + half) % vol_count
     width = 2 * LANES
 
     def peer(k):
-        other_vol = (vol + k // pix_count) % vol_count
-        other_pix = (pix + k % pix_count) % pix_count
-        return other_vol, other_pix
+        return side * half + (place + k // pix_count) % half, (pix + k % pix_count) % pix_count
 
     barrier = pltpu.get_barrier_semaphore()
 
@@ -188,155 +185,172 @@
         pl.semaphore_signal(barrier, inc=1, device_id=peer(k), device_id_type=MESH)
         return unused
 
-    lax.fori_loop(1, device_count, greet, 0)
-    pl.semaphore_wait(barrier, device_count - 1)
-
-    def ids_copy(k):
+    pl.semaphore_signal(barrier, inc=1, device_id=(across, pix), device_id_type=MESH)
+    lax.fori_loop(1, near_count, greet, 0)
+    pl.semaphore_wait(barrier, near_count)
+
+    def final(stage, other_vol, other_pix):
+        return (other_vol + half * (1 - stage)) % vol_count * pix_count + other_pix
+
+    def ids_copy(stage, k):
         other_vol, other_pix = peer(k)
         return pltpu.make_async_remote_copy(
-            src_ref=ids_hbm.at[other_vol * pix_count + other_pix], dst_ref=ids.at[me],
-            send_sem=ids_send.at[k], recv_sem=ids_recv.at[k],
+            src_ref=ids_hbm.at[final(stage, other_vol, other_pix)], dst_ref=ids.at[stage, mine],
+            send_sem=ids_send.at[stage, k], recv_sem=ids_recv.at[stage, k],
             device_id=(other_vol, other_pix), device_id_type=MESH,
         )
 
-    def rows_copy(k):
+    def rows_copy(stage, k):
         other_vol, other_pix = peer(k)
         return pltpu.make_async_remote_copy(
-            src_ref=out_hbm.at[pl.ds((other_vol * pix_count + other_pix) * cap, cap)],
-            dst_ref=arrived.at[pl.ds(me * cap, cap)],
-            send_sem=send_sem.at[k], recv_sem=recv_sem.at[k],
+            src_ref=out_hbm.at[pl.ds(final(stage, other_vol, other_pix) * cap, cap)],
+            dst_ref=arrived.at[stage, pl.ds(mine * cap, cap)],
+            send_sem=send_sem.at[stage, k], recv_sem=recv_sem.at[stage, k],
             device_id=(other_vol, other_pix), device_id_type=MESH,
         )
 
-    def send(k, unused):
-        ids_copy(k).start()
-        rows_copy(k).start()
-        return unused
-
-    lax.fori_loop(1, device_count, send, 0)
-    local_ids = pltpu.make_async_copy(ids_hbm.at[me], ids.at[me], local_sem.at[0])
-    local_rows = pltpu.make_async_copy(
-        out_hbm.at[pl.ds(me * cap, cap)], arrived.at[pl.ds(me * cap, cap)], local_sem.at[1]
-    )
-    local_ids.start()
-    local_rows.start()
-    local_ids.wait()
-    local_rows.wait()
+    def local_copies(stage):
+        own = final(stage, vol, pix)
+        return (
+            pltpu.make_async_copy(ids_hbm.at[own], ids.at[stage, mine], local_sem.at[stage, 0]),
+            pltpu.make_async_copy(
+                out_hbm.at[pl.ds(own * cap, cap)], arrived.at[stage, pl.ds(mine * cap, cap)],
+                local_sem.at[stage, 1],
+            ),
+        )
+
+    for stage in range(2):
+
+        def send(k, unused):
+            ids_copy(stage, k).start()
+            rows_copy(stage, k).start()
+            return unused
+
+        for copy in local_copies(stage):
+            copy.start()
+        lax.fori_loop(1, near_count, send, 0)
 
     group = pix_count * cap
     share = LANES // cap
+    lane_part = iota((1, LANES), 1) // cap
+
+    def sum_up(stage, target):
+        for copy in local_copies(stage):
+            copy.wait()
+        target[...] = jnp.zeros((owned_most, width), F32)
+
+        def receive(i, unused):
+            def one(j, unused):
+                k = i * pix_count + j
+                ids_copy(stage, k).wait_recv()
+                rows_copy(stage, k).wait_recv()
+                return unused
+
+            lax.fori_loop(jnp.where(i == 0, 1, 0), pix_count, one, 0)
+            sender = (place + half - i) % half
+            pieces = []
+            for tau in range(group // LANES):
+                piece = jnp.full((1, LANES), -1, I32)
+                for g in range(share):
+                    line = ids[stage, sender * pix_count + tau * share + g]
+                    piece = jnp.where(lane_part == g, line[0:1], piece)
+                pieces.append(piece)
+            rows = jnp.concatenate(pieces, axis=1) if len(pieces) > 1 else pieces[0]
+            places = onehot(iota((owned_most, group), 0) == rows)
+            start = pl.multiple_of(sender * group, group)
+            moved = dot(places, halves(arrived[stage, pl.ds(start, group), :]))
+            target[...] += moved[:, :width] + moved[:, width:]
+            return unused
+
+        lax.fori_loop(0, half, receive, 0)
+
+    piece_count = mid_send.shape[0]
+    piece_rows = owned_most // piece_count
+
+    def part(q):
+        return pl.ds(q * piece_rows, piece_rows)
+
+    def mid_copy(q):
+        return pltpu.make_async_remote_copy(
+            src_ref=sums.at[part(q)], dst_ref=crossed.at[part(q)],
+            send_sem=mid_send.at[q], recv_sem=mid_recv.at[q],
+            device_id=(across, pix), device_id_type=MESH,
+        )
+
+    sum_up(0, sums)
+    for q in range(piece_count):
+        mid_copy(q).start()
     own = gathered.at[pix]
-    own[...] = jnp.zeros((owned_most, width), F32)
-    lane_part = iota((1, LANES), 1) // cap
-
-    def receive(i, unused):
-        def one(j, unused):
-            k = i * pix_count + j
-            ids_copy(k).wait_recv()
-            rows_copy(k).wait_recv()
-            return unused
-
-        lax.fori_loop(jnp.where(i == 0, 1, 0), pix_count, one, 0)
-        sender = (vol + vol_count - i) % vol_count
-        pieces = []
-        for tau in range(group // LANES):
-            piece = jnp.full((1, LANES), -1, I32)
-            for g in range(share):
-                line = ids[sender * pix_count + tau * share + g]
-                piece = jnp.where(lane_part == g, line[0:1], piece)
-            pieces.append(piece)
-        rows = jnp.concatenate(pieces, axis=1) if len(pieces) > 1 else pieces[0]
-        places = onehot(iota((owned_most, group), 0) == rows)
-        start = pl.multiple_of(sender * group, group)
-        moved = dot(places, halves(arrived[pl.ds(start, group), :]))
-        own[...] += moved[:, :width] + moved[:, width:]
-        return unused
-
-    lax.fori_loop(0, vol_count, receive, 0)
+    sum_up(1, own)
 
     core = pix % 2
     sibling = (vol, pix - core + (1 - core))
-    far_count = pix_count // 2 - 1
-    quarter_count = far_send.shape[1]
-    quarter = owned_most // quarter_count
+    others = range(1, pix_count // 2)
 
     def far_copy(k, q):
-        to = (pix + 2 * k) % pix_count
-        rows = pl.ds(q * quarter, quarter)
-        return pltpu.make_async_remote_copy(
-            src_ref=gathered.at[pix, rows], dst_ref=gathered.at[pix, rows],
+        return pltpu.make_async_remote_copy(
+            src_ref=gathered.at[pix, part(q)], dst_ref=gathered.at[pix, part(q)],
             send_sem=far_send.at[k, q], recv_sem=far_recv.at[k, q],
-            device_id=(vol, to), device_id_type=MESH,
+            device_id=(vol, (pix + 2 * k) % pix_count), device_id_type=MESH,
         )
 
     def pass_copy(k, q):
         source = (pix + pix_count - 2 * k) % pix_count
-        rows = pl.ds(q * quarter, quarter)
-        return pltpu.make_async_remote_copy(
-            src_ref=gathered.at[source, rows], dst_ref=gathered.at[source, rows],
+        return pltpu.make_async_remote_copy(
+            src_ref=gathered.at[source, part(q)], dst_ref=gathered.at[source, part(q)],
             send_sem=pass_send.at[k, q], recv_sem=pass_recv.at[k, q],
             device_id=sibling, device_id_type=MESH,
         )
 
-    own_copy = pltpu.make_async_remote_copy(
-        src_ref=gathered.at[pix], dst_ref=gathered.at[pix],
-        send_sem=own_send.at[0], recv_sem=own_recv.at[0],
-        device_id=sibling, device_id_type=MESH,
-    )
-    for q in range(quarter_count):
-        for k in range(1, far_count + 1):
-            far_copy(k, q).start()
-    own_copy.start()
-    owned_ref[...] = own[...]
-
-    def gather(p, start):
-        data = halves(gathered[p])
-
-        def one(h, unused):
-            at = pl.ds(pl.multiple_of(h * LANES, LANES), LANES)
-            codes = code_ref[at, :] - p * owned_most
-            places = jnp.concatenate(
-                [
-                    onehot(codes == iota((LANES, LANES), 1) + r * LANES)
-                    for r in range(owned_most // LANES)
-                ],
-                axis=1,
-            )
-            moved = dot(places, data)
-            moved = moved[:, :width] + moved[:, width:]
-            if start:
-                shell_ref[at, :] = moved
-            else:
-                shell_ref[at, :] += moved
-            return unused
-
-        lax.fori_loop(0, block_tiles // LANES, one, 0)
-
-    gather(pix, True)
-    for q in range(quarter_count):
-        for k in range(1, far_count + 1):
+    def own_copy(q):
+        return pltpu.make_async_remote_copy(
+            src_ref=gathered.at[pix, part(q)], dst_ref=gathered.at[pix, part(q)],
+            send_sem=own_send.at[q], recv_sem=own_recv.at[q],
+            device_id=sibling, device_id_type=MESH,
+        )
+
+    def relay(q):
+        for k in others:
             far_copy(k, q).wait_recv()
             pass_copy(k, q).start()
-    own_copy.wait_recv()
-    gather(sibling[1], False)
-    for k in range(1, far_count + 1):
-        gather((pix + pix_count - 2 * k) % pix_count, False)
-        for q in range(quarter_count):
-            pass_copy(k, q).wait_recv()
-        gather((sibling[1] + pix_count - 2 * k) % pix_count, False)
-
-    own_copy.wait_send()
-    for q in range(quarter_count):
-        for k in range(1, far_count + 1):
+
+    for q in range(piece_count):
+        mid_copy(q).wait_recv()
+        whole = own[part(q), :] + crossed[part(q), :]
+        own[part(q), :] = whole
+        owned_ref[part(q), :] = whole
+        for k in others:
+            far_copy(k, q).start()
+        own_copy(q).start()
+        if q:
+            relay(q - 1)
+    relay(piece_count - 1)
+    for q in range(piece_count):
+        own_copy(q).wait()
+        mid_copy(q).wait_send()
+        for k in others:
             far_copy(k, q).wait_send()
-            pass_copy(k, q).wait_send()
-
-    def sent(k, unused):
-        ids_copy(k).wait_send()
-        rows_copy(k).wait_send()
+            pass_copy(k, q).wait()
+
+    def gather(i, unused):
+        lines = []
+        for j in range(8):
+            code = code_ref[i * 8 + j]
+            source = code // owned_most
+            lines.append(gathered[source, pl.ds(code - source * owned_most, 1), :])
+        shell_ref[pl.ds(pl.multiple_of(i * 8, 8), 8), :] = jnp.concatenate(lines, axis=0)
         return unused
 
-    lax.fori_loop(1, device_count, sent, 0)
+    lax.fori_loop(0, block_tiles // 8, gather, 0, unroll=2)
+
+    for stage in range(2):
+
+        def sent(k, unused):
+            ids_copy(stage, k).wait_send()
+            rows_copy(stage, k).wait_send()
+            return unused
+
+        lax.fori_loop(1, near_count, sent, 0)
 
 
 def shards(kernel, pressure, velocity, entry_slot, slot_tile, tile_owner):
@@ -364,7 +378,7 @@
         out_shape=(
             jax.ShapeDtypeStruct((device_count * cap, width), F32),
             jax.ShapeDtypeStruct((device_count, 8, LANES), I32),
-            jax.ShapeDtypeStruct((block_tiles, LANES), I32),
+            jax.ShapeDtypeStruct((block_tiles // LANES, LANES), I32),
         ),
         in_specs=[smem, smem, anywhere, vmem, vmem, vmem, vmem, vmem],
         out_specs=(vmem, vmem, vmem),
@@ -374,6 +388,7 @@
             pltpu.VMEM(shape, F32),
             pltpu.VMEM((slots + WINDOW, width), F32),
             pltpu.VMEM((slots, 2 * width), BF16),
+            pltpu.VMEM((tiles // LANES, LANES), I32),
             dma((4,)),
         ],
         name="prepare",
@@ -382,28 +397,30 @@
         entry_slot.reshape(shape), slot_tile, tile_owner.reshape(tiles // LANES, LANES),
     )
 
-    quarters = 4
+    pieces = 4
     chips = pix_count // 2
+    near = device_count // 2
     return pl.pallas_call(
         functools.partial(exchange, dims),
         out_shape=(
             jax.ShapeDtypeStruct((owned_most, width), F32),
             jax.ShapeDtypeStruct((block_tiles, width), F32),
         ),
-        in_specs=[anywhere, anywhere, vmem],
+        in_specs=[anywhere, anywhere, smem],
         out_specs=(vmem, vmem),
         scratch_shapes=[
-            pltpu.VMEM((device_count * cap, width), F32),
-            pltpu.VMEM((device_count, 8, LANES), I32),
+            pltpu.VMEM((2, near * cap, width), F32),
+            pltpu.VMEM((2, near, 8, LANES), I32),
+            pltpu.VMEM((owned_most, width), F32),
+            pltpu.VMEM((owned_most, width), F32),
             pltpu.VMEM((pix_count, owned_most, width), F32),
-            dma((device_count,)), dma((device_count,)), dma((device_count,)), dma((device_count,)),
-            dma((2,)), dma((1,)), dma((1,)),
-            dma((chips, quarters)), dma((chips, quarters)),
-            dma((chips, quarters)), dma((chips, quarters)),
+            dma((2, near)), dma((2, near)), dma((2, near)), dma((2, near)),
+            dma((2, 2)), dma((pieces,)), dma((pieces,)), dma((pieces,)), dma((pieces,)),
+            dma((chips, pieces)), dma((chips, pieces)), dma((chips, pieces)), dma((chips, pieces)),
         ],
         compiler_params=pltpu.CompilerParams(collective_id=0, has_side_effects=True),
         name="exchange",
-    )(outgoing, ids, codes)
+    )(outgoing, ids, codes.reshape(block_tiles))
 
 
 def solution(mesh):

time: 99.2 us -> 87.6 us (0.88)
  Pallas kernels: 90.5 us -> 79 us
    pallas_call x1, Pallas kernels: 78.3 us -> 66.8 us  [shards(): pl.pallas_call(functools.partial(exchange, dims), out_shape=(jax.ShapeDty...]
where the time goes in v2:
time: 87.6 us; the launch traced here: 87.2 us
  Pallas kernels  79 us (90%)
  local copies, waits for them, and re-layouts  5.41 us (6%)
  other arithmetic  2.2 us (3%)
    pallas_call x1, Pallas kernels, shards(): pl.pallas_call(functools.partial(exchange, dims), out_shape=(jax.ShapeDty...  66.8 us
    pallas_call x1, Pallas kernels, shards(): pl.pallas_call(functools.partial(prepare, dims), out_shape=(jax.ShapeDtyp...  12.2 us
    unnamed x5, local copies, waits for them, and re-layouts  5.31 us

profile of v2, /device:TPU:29, one launch (start us, length us, event | category | flops | bytes accessed | tf_op | source)
XLA Modules:
  0.0 87.2 jit_solution(1033021302380785238)
XLA Ops:
  0.6 0.5 broadcast.12
  1.1 1.6 %reduce.3 = s32[16384]{0:T(1024)S(1)} reduce(s32[1,16384]{1,0:T(1,128)} %param.9, s32[]{:T(128)} %broadcast.12), dimensions={0}, to_apply=%param.9.reduce_sub_computation.3 | reduce | bytes 131076 | tf_op args[3]
  2.8 0.1 fusion.1
  2.9 0.6 copy.11
  3.5 0.1 copy.10
  3.6 0.6 fusion.base_ref
  4.1 12.2 %prepare.1 = (f32[2048,256]{1,0:T(8,128)}, s32[32,8,128]{2,1,0:T(8,128)}, s32[8,128]{1,0:T(8,128)}) custom-call(s32[64]{0:T(128)} %fusion.base_ref, s32[64]{0:T(128)} %bitcast.21, bf16[16384,128]{1,0:T(8,128)(2,1)} %kern_hbm.1, bf16[128,128]{1,0:T(8,128)(2,1)} %bitcast.17, bf16[128,128]{1,0:T(8,128)(2,1)} %bitcast.18, s32[128,128]{1,0:T(8,128)} %bitcast.16, ...), custom_call_target="tpu_custom_call" | custom-call | tf_op jit(solution)/shard_map/prepare/pallas_call | solution.py:376
  16.3 66.8 %exchange.1 = (f32[512,256]{1,0:T(8,128)}, f32[1024,256]{1,0:T(8,128)}) custom-call(f32[2048,256]{1,0:T(8,128)} %get-tuple-element.5.out_hbm, s32[32,8,128]{2,1,0:T(8,128)} %get-tuple-element.6.ids_hbm, s32[1024]{0:T(1024)} %bitcast.20), custom_call_target="tpu_custom_call" | custom-call | tf_op jit(solution)/shard_map/exchange/pallas_call | solution.py:403
  83.1 1.9 %copy.14 = f32[512,256]{1,0:T(8,128)} copy(f32[512,256]{1,0:T(8,128)} %get-tuple-element.12) | data formatting | bytes 1048576
  85.0 2.3 %copy.15 = f32[1024,256]{1,0:T(8,128)} copy(f32[1024,256]{1,0:T(8,128)} %get-tuple-element.13) | data formatting | bytes 2097152
  (1 shorter events, 0.0 us)
